TPU v7x, 8 devices: a whole 2x2x1 slice. The times are simulated.
8 devices in a mesh: ens: 1 (over z), part: 2 (over y), feat: 4 (over x, core).
Axes of the slice: x: 2, y: 2, z: 1, core: 2. Of those that a mesh axis runs over, the one named last changes fastest.
Arguments:
- particles: float32 [4096, 2048], P(('ens', 'part'), 'feat')
- prec_diag: float32 [2048], P(('ens', 'feat'))
- target_mean: float32 [2048], P(('ens', 'feat'))
- low_factor: bfloat16 [2048, 16], P(('ens', 'feat'))
Outputs:
- output: float32 [4096, 2048], P(('ens', 'part'), 'feat')
All inputs are finite; a program needn't handle non-finite values.
Results may differ from a plain program's by a relative error of at most 0.00403875.
Values are sent between devices in bfloat16 or wider.
A program may use at most 1 GiB of HBM per device.

v0:
```python
import math
import jax
import jax.numpy as jnp
from jax import lax
from jax.sharding import PartitionSpec as P

NUM_STEPS = 3


def solution(mesh):
    part_size = mesh.shape["part"]
    feat_size = mesh.shape["feat"]

    def local_steps(local_theta, prec_loc, mean_loc, factor_loc):
        rows_loc, feat_loc = local_theta.shape
        n_total = rows_loc * part_size
        feat_total = feat_loc * feat_size
        kern_width = 2.0 * feat_total / math.log(n_total)
        step_size = 0.15 * n_total * feat_total / math.log(n_total)
        row_start = lax.axis_index("part") * rows_loc
        cur_theta = local_theta
        for step_idx in range(NUM_STEPS):
            x_dev = cur_theta - mean_loc[None, :]
            proj_part = jnp.dot(x_dev.astype(jnp.bfloat16), factor_loc, preferred_element_type=jnp.float32)
            proj_low = lax.psum(proj_part, "feat")
            low_term = jnp.einsum("nr,dr->nd", proj_low.astype(jnp.bfloat16), factor_loc, preferred_element_type=jnp.float32)
            grad_b = (-(x_dev * prec_loc[None, :] + low_term)).astype(jnp.bfloat16)
            theta_b = cur_theta.astype(jnp.bfloat16)
            theta_all = lax.all_gather(theta_b, "part", axis=0, tiled=True)
            gram_part = jnp.einsum("nd,md->nm", theta_b, theta_all, preferred_element_type=jnp.float32)
            sq_part = jnp.einsum("md,md->m", theta_all, theta_all, preferred_element_type=jnp.float32)
            gram_rows, sq_norm = lax.psum((gram_part, sq_part), "feat")
            sq_own = lax.dynamic_slice_in_dim(sq_norm, row_start, rows_loc)
            sq_dist = jnp.maximum(sq_own[:, None] + sq_norm[None, :] - 2.0 * gram_rows, 0.0)
            kern_b = jnp.exp(-sq_dist / kern_width).astype(jnp.bfloat16)
            row_mass = jnp.sum(kern_b, axis=1, dtype=jnp.float32)
            grad_all = lax.all_gather(grad_b, "part", axis=0, tiled=True)
            drive_term = jnp.dot(kern_b, grad_all, preferred_element_type=jnp.float32)
            pull_term = jnp.dot(kern_b, theta_all, preferred_element_type=jnp.float32)
            update_dir = (drive_term + (2.0 / kern_width) * (row_mass[:, None] * theta_b.astype(jnp.float32) - pull_term)) / n_total
            cur_theta = cur_theta + step_size * update_dir
        return cur_theta

    row_spec = P(("ens", "part"), "feat")
    vec_spec = P(("ens", "feat"))
    fac_spec = P(("ens", "feat"), None)
    return jax.shard_map(local_steps, mesh=mesh, in_specs=(row_spec, vec_spec, vec_spec, fac_spec), out_specs=row_spec, check_vma=False)
```

profile of v0, /device:TPU:0, one launch (start us, length us, event | category | flops | bytes accessed | tf_op | source)
XLA Modules:
  0.0 2202.2 jit_solution(3021779310028017341)
XLA Ops:
  6.5 3.8 convert_element_type.63
  10.4 57.1 %all-gather.7.cloned.1.call-done = bf16[4096,512]{1,0:T(8,128)(2,1)} async-done(((bf16[2048,512]{1,0:T(8,128)(2,1)}), bf16[4096,512]{1,0:T(8,128)(2,1)}) %all-gather.7.cloned.1.call-update) | async-done | bytes 4194320 | tf_op jit(solution)/shard_map/all_gather | solution.py:29
  67.5 18.1 fusion.14
  86.3 3.0 fusion.3
  90.7 42.0 %all-reduce.15 = (f32[4096]{0:T(1024)S(1)}, bf16[2048,16]{1,0:T(8,128)(2,1)S(1)}) all-reduce(f32[4096]{0:T(1024)S(1)} %fusion.2, f32[2048,16]{1,0:T(8,128)S(1)} %fusion.3), channel_id=1, replica_groups=mesh['ens'=1,'part'=2,'feat'=4] {'feat'}, use_global_device_ids=true, to_apply=%region_0.0 | all-reduce | flops 36864 | bytes 229376 | tf_op jit(solution)/shard_map/psum | solution.py:32
  132.7 4.2 negate_convert_fusion.2
  137.2 518.4 %all-reduce.10.cloned.1.call-done = f32[2048,4096]{1,0:T(8,128)} async-done(((f32[2048,4096]{1,0:T(8,128)}), f32[2048,4096]{1,0:T(8,128)}) %all-reduce.10.cloned.1.call-update) | async-done | bytes 33554448 | tf_op jit(solution)/shard_map/psum | solution.py:32
  655.6 22.1 %convert_reduce_fusion.2 = (f32[2048]{0:T(1024)S(1)}, bf16[2048,4096]{1,0:T(8,128)(2,1)}) fusion(f32[2048,4096]{1,0:T(8,128)} %all-reduce.10.cloned.1.call-done, f32[4096]{0:T(1024)S(1)} %get-tuple-element.9, f32[2048]{0:T(1024)S(1)} %dynamic_slice.9), kind=kLoop, calls=%fused_computation.4 | loop fusion | flops 75495424 | bytes 50364416 | tf_op jit(solution)/shard_map/reduce_sum | solution.py:36
  677.7 33.7 %all-gather.9.cloned.1.call-done = bf16[4096,512]{1,0:T(8,128)(2,1)} async-done(((bf16[2048,512]{1,0:T(8,128)(2,1)}), bf16[4096,512]{1,0:T(8,128)(2,1)}) %all-gather.9.cloned.1.call-update) | async-done | bytes 4194320 | tf_op jit(solution)/shard_map/all_gather | solution.py:37
  711.4 13.3 fusion.16
  724.7 14.6 fusion.12
  739.4 54.3 %all-gather.11.cloned.1.call-done = bf16[4096,512]{1,0:T(8,128)(2,1)} async-done(((bf16[2048,512]{1,0:T(8,128)(2,1)}), bf16[4096,512]{1,0:T(8,128)(2,1)}) %all-gather.11.cloned.1.call-update) | async-done | bytes 4194320 | tf_op jit(solution)/shard_map/all_gather | solution.py:29
  793.7 17.8 fusion.17
  811.6 3.0 fusion.4
  815.9 42.2 %all-reduce.16 = (f32[4096]{0:T(1024)S(1)}, bf16[2048,16]{1,0:T(8,128)(2,1)S(1)}) all-reduce(f32[4096]{0:T(1024)S(1)} %fusion.1, f32[2048,16]{1,0:T(8,128)S(1)} %fusion.4), channel_id=1, replica_groups=mesh['ens'=1,'part'=2,'feat'=4] {'feat'}, use_global_device_ids=true, to_apply=%region_4.0 | all-reduce | flops 36864 | bytes 229376 | tf_op jit(solution)/shard_map/psum | solution.py:32
  858.1 4.3 negate_convert_fusion.1
  862.5 518.9 %all-reduce.12.cloned.1.call-done = f32[2048,4096]{1,0:T(8,128)} async-done(((f32[2048,4096]{1,0:T(8,128)}), f32[2048,4096]{1,0:T(8,128)}) %all-reduce.12.cloned.1.call-update) | async-done | bytes 33554448 | tf_op jit(solution)/shard_map/psum | solution.py:32
  1381.4 22.1 %convert_reduce_fusion.1 = (f32[2048]{0:T(1024)S(1)}, bf16[2048,4096]{1,0:T(8,128)(2,1)}) fusion(f32[2048,4096]{1,0:T(8,128)} %all-reduce.12.cloned.1.call-done, f32[4096]{0:T(1024)S(1)} %get-tuple-element.7, f32[2048]{0:T(1024)S(1)} %dynamic_slice.10), kind=kLoop, calls=%fused_computation.2 | loop fusion | flops 75495424 | bytes 50364416 | tf_op jit(solution)/shard_map/reduce_sum | solution.py:36
  1403.6 33.5 %all-gather.13.cloned.1.call-done = bf16[4096,512]{1,0:T(8,128)(2,1)} async-done(((bf16[2048,512]{1,0:T(8,128)(2,1)}), bf16[4096,512]{1,0:T(8,128)(2,1)}) %all-gather.13.cloned.1.call-update) | async-done | bytes 4194320 | tf_op jit(solution)/shard_map/all_gather | solution.py:37
  1437.1 15.1 fusion.18
  1452.2 15.2 fusion.13
  1467.7 54.0 %all-gather.15.cloned.1.call-done = bf16[4096,512]{1,0:T(8,128)(2,1)} async-done(((bf16[2048,512]{1,0:T(8,128)(2,1)}), bf16[4096,512]{1,0:T(8,128)(2,1)}) %all-gather.15.cloned.1.call-update) | async-done | bytes 4194320 | tf_op jit(solution)/shard_map/all_gather | solution.py:29
  1521.7 17.8 fusion.19
  1539.6 3.0 fusion.5
  1543.0 0.9 fusion
  1543.9 42.0 %all-reduce.17 = (f32[4096]{0:T(1024)S(1)}, bf16[2048,16]{1,0:T(8,128)(2,1)S(1)}) all-reduce(f32[4096]{0:T(1024)S(1)} %fusion, f32[2048,16]{1,0:T(8,128)S(1)} %fusion.5), channel_id=1, replica_groups=mesh['ens'=1,'part'=2,'feat'=4] {'feat'}, use_global_device_ids=true, to_apply=%region_8.0 | all-reduce | flops 36864 | bytes 229376 | tf_op jit(solution)/shard_map/psum | solution.py:32
  1585.9 4.3 negate_convert_fusion
  1590.3 519.2 %all-reduce.14.cloned.1.call-done = f32[2048,4096]{1,0:T(8,128)} async-done(((f32[2048,4096]{1,0:T(8,128)}), f32[2048,4096]{1,0:T(8,128)}) %all-reduce.14.cloned.1.call-update) | async-done | bytes 33554448 | tf_op jit(solution)/shard_map/psum | solution.py:32
  2109.4 22.1 %convert_reduce_fusion = (f32[2048]{0:T(1024)S(1)}, bf16[2048,4096]{1,0:T(8,128)(2,1)}) fusion(f32[2048,4096]{1,0:T(8,128)} %all-reduce.14.cloned.1.call-done, f32[4096]{0:T(1024)S(1)} %get-tuple-element.5, f32[2048]{0:T(1024)S(1)} %dynamic_slice.11), kind=kLoop, calls=%fused_computation | loop fusion | flops 75495424 | bytes 50364416 | tf_op jit(solution)/shard_map/reduce_sum | solution.py:36
  2131.6 33.7 %all-gather.17.cloned.1.call-done = bf16[4096,512]{1,0:T(8,128)(2,1)} async-done(((bf16[2048,512]{1,0:T(8,128)(2,1)}), bf16[4096,512]{1,0:T(8,128)(2,1)}) %all-gather.17.cloned.1.call-update) | async-done | bytes 4194320 | tf_op jit(solution)/shard_map/all_gather | solution.py:37
  2165.3 15.1 fusion.20
  2180.3 14.9 multiply_add_fusion
  (51 shorter events, 4.6 us)
Async XLA Ops:
  6.5 79.2 %copy-start = (bf16[512,16]{0,1:T(8,128)(2,1)S(1)}, bf16[512,16]{0,1:T(8,128)(2,1)}, u32[]{:S(2)}) copy-start(bf16[512,16]{0,1:T(8,128)(2,1)} %param.7) | copy-start | bytes 49156
  6.5 61.0 %all-gather.7.cloned.1.call-start = ((), (), s32[]{:S(2)}) async-start(), calls=%async_computation | async-start | bytes 6291456 | tf_op jit(solution)/shard_map/all_gather | solution.py:29
  10.3 645.2 %all-reduce.10.cloned.1.call-start = ((), (), s32[]{:S(2)}) async-start(), calls=%async_computation.1 | async-start | bytes 67108864 | tf_op jit(solution)/shard_map/psum | solution.py:32
  85.6 0.7 copy-start.12
  85.7 47.0 %copy-start.13 = (f32[512]{0:T(512)S(1)}, f32[512]{0:T(512)}, u32[]{:S(2)}) copy-start(f32[512]{0:T(512)} %param.5) | copy-start | bytes 6148
  85.7 625.7 %all-gather.9.cloned.1.call-start = ((), (), s32[]{:S(2)}) async-start(), calls=%async_computation.2 | async-start | bytes 6291456 | tf_op jit(solution)/shard_map/all_gather | solution.py:37
  86.3 3.4 copy-start.4
  137.0 656.8 %all-gather.11.cloned.1.call-start = ((), (), s32[]{:S(2)}) async-start(), calls=%async_computation.3 | async-start | bytes 6291456 | tf_op jit(solution)/shard_map/all_gather | solution.py:29
  711.4 13.3 copy-start.1
  711.4 13.3 copy-start.5
  739.4 642.0 %all-reduce.12.cloned.1.call-start = ((), (), s32[]{:S(2)}) async-start(), calls=%async_computation.4 | async-start | bytes 67108864 | tf_op jit(solution)/shard_map/psum | solution.py:32
  811.5 625.6 %all-gather.13.cloned.1.call-start = ((), (), s32[]{:S(2)}) async-start(), calls=%async_computation.5 | async-start | bytes 6291456 | tf_op jit(solution)/shard_map/all_gather | solution.py:37
  811.6 3.5 copy-start.6
  862.5 659.3 %all-gather.15.cloned.1.call-start = ((), (), s32[]{:S(2)}) async-start(), calls=%async_computation.6 | async-start | bytes 6291456 | tf_op jit(solution)/shard_map/all_gather | solution.py:29
  1437.1 15.1 copy-start.2
  1437.1 15.1 copy-start.7
  1437.1 15.1 copy-start.10
  1467.4 642.0 %all-reduce.14.cloned.1.call-start = ((), (), s32[]{:S(2)}) async-start(), calls=%async_computation.7 | async-start | bytes 67108864 | tf_op jit(solution)/shard_map/psum | solution.py:32
  1539.5 625.7 %all-gather.17.cloned.1.call-start = ((), (), s32[]{:S(2)}) async-start(), calls=%async_computation.8 | async-start | bytes 6291456 | tf_op jit(solution)/shard_map/all_gather | solution.py:37
  1539.6 3.5 copy-start.8
  2165.2 15.1 copy-start.3
  2165.2 15.1 copy-start.9
  2165.3 15.1 copy-start.11
Sparse Core Ops, SparseCore 0:
  10.5 57.0 all-gather.6
  85.8 569.7 all-reduce.9
  657.1 54.2 all-gather.8
  739.5 54.1 all-gather.10
  811.6 569.7 all-reduce.11
  1382.8 54.2 all-gather.12
  1467.5 54.1 all-gather.14
  1539.7 569.7 all-reduce.13
  2111.0 54.2 all-gather.16
where the time goes:
time: 2210 us; the launch traced here: 2200 us
  waiting for transfers between devices  1820 us (82%)
  matrix products  164 us (7%)
  blocking collectives  126 us (6%)
  other arithmetic  72.8 us (3%)
    psum x3, waiting for transfers between devices, local_steps(): gram_rows, sq_norm = lax.psum((gram_part, sq_part), 'feat')  1560 us
    all_gather x3, waiting for transfers between devices, local_steps(): theta_all = lax.all_gather(theta_b, 'part', axis=0, tiled=True)  165 us
    psum x3, blocking collectives, local_steps(): gram_rows, sq_norm = lax.psum((gram_part, sq_part), 'feat')  126 us
    all_gather x3, waiting for transfers between devices, local_steps(): grad_all = lax.all_gather(grad_b, 'part', axis=0, tiled=True)  101 us
    reduce_sum x3, other arithmetic, local_steps(): row_mass = jnp.sum(kern_b, axis=1, dtype=jnp.float32)  66.4 us
    dot_general x3, matrix products, local_steps(): jnp.einsum('nd,md->nm', theta_b, theta_all, preferred_element_type=jnp.fl...  53.7 us
    dot_general x3, matrix products, local_steps(): pull_term = jnp.dot(kern_b, theta_all, preferred_element_type=jnp.float32)  44.7 us
  transfers between devices with their start and end apart: 9, of which 9 were waited for; matrix products, arithmetic and copies ran while one was open for 4% of the time, Pallas kernels for 0%

commit v1 on v0

v1 whole, which is shorter than its diff:
```python
import functools
import math
import jax
import jax.numpy as jnp
from jax import lax
from jax.experimental import pallas as pl
from jax.experimental.pallas import tpu as pltpu
from jax.sharding import PartitionSpec as P

NUM_STEPS = 3
CHUNK = 256
WIDE = 512
F32 = jnp.float32
BF16 = jnp.bfloat16
MESH = pl.DeviceIdType.MESH

OWN, SIB, FAR, FAR_SIB = 0, 1, 2, 3
(T_TO_Y, T_TO_X, T_TO_SIB, FAR_TO_X, FAR_TO_SIB, OTHER_TO_SIB, DIAG_TO_SIB,
 A_TO_Y, A_TO_SIB, FAR_A_TO_SIB, Z_TO_X) = range(11)
S_TO_SIB, S_TO_Y, FAR_S_TO_SIB = range(3)
FACTOR_TO_SIB, VECS_TO_SIB = range(2)


def dot_nt(left, right):
    return lax.dot_general(left, right, (((1,), (1,)), ((), ())), preferred_element_type=F32)


def dot_nn(left, right):
    return lax.dot_general(left, right, (((1,), (0,)), ((), ())), preferred_element_type=F32)


def dot_tn(left, right):
    return lax.dot_general(left, right, (((0,), (0,)), ((), ())), preferred_element_type=F32)


def svgd_kernel(n_total, kern_width, step_size, theta_in, vecs_in, factor_in, out, theta, vecs, factor_t,
                tb, ab, zs, sb, srow, mass, send, recv, small_send, small_recv,
                load_sem, give_sem, take_sem, table_send, table_recv):
    rows, feats = theta.shape
    wide = feats // 2
    rank = factor_t.shape[0]
    chunks = rows // CHUNK
    gain = step_size / n_total
    pull_gain = gain * 2.0 / kern_width
    feat = lax.axis_index("feat")
    part = lax.axis_index("part")
    core = lax.rem(feat, 2)
    to_sib = {"feat": feat + 1 - 2 * core}
    to_x = {"feat": lax.rem(feat + 2, 4)}
    to_y = {"part": 1 - part}
    mine = pl.ds(pl.multiple_of(core * wide, wide), wide)
    theirs = pl.ds(pl.multiple_of((1 - core) * wide, wide), wide)

    barrier = pltpu.get_barrier_semaphore()
    for peer in (to_sib, to_x, to_y):
        pl.semaphore_signal(barrier, inc=1, device_id=peer, device_id_type=MESH)

    def span(i):
        return pl.ds(pl.multiple_of(i * CHUNK, CHUNK), CHUNK)

    def half_rows(which, i):
        return pl.ds(pl.multiple_of(which * rows + i * CHUNK, CHUNK), CHUNK)

    def load(i):
        return pltpu.make_async_copy(
            theta_in.at[half_rows(core, i)], theta.at[span(i), mine], load_sem.at[0, i])

    def give(i):
        return pltpu.make_async_remote_copy(
            src_ref=theta_in.at[half_rows(1 - core, i)], dst_ref=theta.at[span(i), mine],
            send_sem=give_sem.at[0, i], recv_sem=take_sem.at[0, i], device_id=to_sib, device_id_type=MESH)

    def store(i):
        return pltpu.make_async_copy(
            theta.at[span(i), mine], out.at[half_rows(core, i)], load_sem.at[1, i])

    def give_back(i):
        return pltpu.make_async_remote_copy(
            src_ref=theta.at[span(i), theirs], dst_ref=out.at[half_rows(core, i)],
            send_sem=give_sem.at[1, i], recv_sem=take_sem.at[1, i], device_id=to_sib, device_id_type=MESH)

    def table(kind):
        src, dst = {
            FACTOR_TO_SIB: (factor_in, factor_t.at[:, mine]),
            VECS_TO_SIB: (vecs_in, vecs.at[:, mine]),
        }[kind]
        return pltpu.make_async_remote_copy(
            src_ref=src, dst_ref=dst, send_sem=table_send.at[kind], recv_sem=table_recv.at[kind],
            device_id=to_sib, device_id_type=MESH)

    def copy(kind, p, i):
        if kind == Z_TO_X:
            return pltpu.make_async_remote_copy(
                src_ref=zs.at[p, 0, :, span(i)], dst_ref=zs.at[p, 1, :, span(i)], send_sem=send.at[p, kind, i],
                recv_sem=recv.at[p, kind, i], device_id=to_x, device_id_type=MESH)
        src, dst, peer = {
            T_TO_Y: (tb.at[p, OWN, 0], tb.at[p, FAR, 0], to_y),
            T_TO_X: (tb.at[p, OWN, 0], tb.at[p, OWN, 1], to_x),
            T_TO_SIB: (tb.at[p, OWN, 0], tb.at[p, SIB, 0], to_sib),
            FAR_TO_X: (tb.at[p, FAR, 0], tb.at[p, FAR, 1], to_x),
            FAR_TO_SIB: (tb.at[p, FAR, 0], tb.at[p, FAR_SIB, 0], to_sib),
            OTHER_TO_SIB: (tb.at[p, OWN, 1], tb.at[p, SIB, 1], to_sib),
            DIAG_TO_SIB: (tb.at[p, FAR, 1], tb.at[p, FAR_SIB, 1], to_sib),
            A_TO_Y: (ab.at[p, OWN], ab.at[p, FAR], to_y),
            A_TO_SIB: (ab.at[p, OWN], ab.at[p, SIB], to_sib),
            FAR_A_TO_SIB: (ab.at[p, FAR], ab.at[p, FAR_SIB], to_sib),
        }[kind]
        return pltpu.make_async_remote_copy(
            src_ref=src.at[span(i)], dst_ref=dst.at[span(i)], send_sem=send.at[p, kind, i],
            recv_sem=recv.at[p, kind, i], device_id=peer, device_id_type=MESH)

    def small(kind, p):
        src, dst, peer = {
            S_TO_SIB: (sb.at[p, OWN], sb.at[p, SIB], to_sib),
            S_TO_Y: (sb.at[p, OWN], sb.at[p, FAR], to_y),
            FAR_S_TO_SIB: (sb.at[p, FAR], sb.at[p, FAR_SIB], to_sib),
        }[kind]
        return pltpu.make_async_remote_copy(
            src_ref=src, dst_ref=dst, send_sem=small_send.at[p, kind],
            recv_sem=small_recv.at[p, kind], device_id=peer, device_id_type=MESH)

    def each_chunk(body):
        lax.fori_loop(0, chunks, lambda i, c: (body(i), c)[1], 0)

    def emit(p, i):
        here = theta[span(i), :]
        here_b = here.astype(BF16)
        tb[p, OWN, 0, span(i), :] = here_b
        x_dev = here - vecs[1:2, :]
        near = here_b.astype(F32)
        norm = jnp.broadcast_to(jnp.sum(near * near, axis=1, keepdims=True), (CHUNK, 128))
        zs[p, 0, 0:rank, span(i)] = dot_nt(factor_t[...], x_dev.astype(BF16))
        zs[p, 0, rank:rank + 8, span(i)] = jnp.transpose(norm)[0:8, :]
        for kind in (Z_TO_X, T_TO_Y, T_TO_X, T_TO_SIB):
            copy(kind, p, i).start()

    def total_norm(p, i):
        copy(Z_TO_X, p, i).wait_recv()
        sb[p, OWN, :, span(i)] = zs[p, 0, rank:rank + 8, span(i)] + zs[p, 1, rank:rank + 8, span(i)]

    def drive(p, i):
        here = theta[span(i), :]
        z_low = zs[p, 0, 0:rank, span(i)] + zs[p, 1, 0:rank, span(i)]
        low_term = dot_tn(z_low.astype(BF16), factor_t[...])
        x_dev = here - vecs[1:2, :]
        ab[p, OWN, span(i), :] = (-(x_dev * vecs[0:1, :] + low_term)).astype(BF16)
        copy(A_TO_Y, p, i).start()
        copy(A_TO_SIB, p, i).start()

    def row_norm(p, i):
        near = tb[p, OWN, 0, span(i), :].astype(F32)
        other = tb[p, OWN, 1, span(i), :].astype(F32)
        total = jnp.sum(near * near + other * other, axis=1, keepdims=True)
        srow[span(i), :] = jnp.broadcast_to(total, (CHUNK, 128))

    def tile(p, i, blocks, start, width):
        cols = pl.ds(pl.multiple_of(start, width), width)
        parts = []
        for block in blocks:
            gram = dot_nt(tb[p, OWN, 0, span(i), :], tb[p, block, 0, cols, :])
            gram = gram + dot_nt(tb[p, OWN, 1, span(i), :], tb[p, block, 1, cols, :])
            sq_dist = jnp.maximum(srow[span(i), 0:1] + sb[p, block, 0:1, cols] - 2.0 * gram, 0.0)
            parts.append(jnp.exp(sq_dist * (-1.0 / kern_width)).astype(BF16))
        kern = jnp.concatenate(parts, axis=1)
        heavy = kern.astype(F32)
        lanes = heavy[:, 0:128]
        for q in range(1, kern.shape[1] // 128):
            lanes = lanes + heavy[:, q * 128:(q + 1) * 128]
        mass[span(i), :] += lanes
        push = dot_nn(kern, jnp.concatenate([ab[p, block, cols, :] for block in blocks], axis=0))
        pull = dot_nn(kern, jnp.concatenate([tb[p, block, 0, cols, :] for block in blocks], axis=0))
        theta[span(i), :] += gain * push - pull_gain * pull

    def near_group(p, block):
        per_row = rows // WIDE

        def body(q):
            tile(p, q // per_row, (block,), lax.rem(q, per_row) * WIDE, WIDE)
        lax.fori_loop(0, chunks * per_row, lambda q, c: (body(q), c)[1], 0)

    def far_pair(p, i, j):
        tile(p, i, (FAR, FAR_SIB), j * CHUNK, CHUNK)

    def far_arrive(p, j):
        copy(FAR_TO_X, p, j).wait_recv()
        copy(DIAG_TO_SIB, p, j).start()
        copy(A_TO_Y, p, j).wait_recv()
        copy(FAR_A_TO_SIB, p, j).start()

    def far_ready(p, j):
        copy(FAR_TO_SIB, p, j).wait_recv()
        copy(DIAG_TO_SIB, p, j).wait_recv()
        copy(FAR_A_TO_SIB, p, j).wait_recv()

    each_chunk(lambda i: load(i).start())
    vecs[:, mine] = vecs_in[...]
    factor_t[:, mine] = factor_in[...]
    pl.semaphore_wait(barrier, 3)
    for kind in (FACTOR_TO_SIB, VECS_TO_SIB):
        table(kind).start()
    each_chunk(lambda i: give(i).start())
    for kind in (FACTOR_TO_SIB, VECS_TO_SIB):
        table(kind).wait_recv()

    def begin(i):
        load(i).wait()
        give(i).wait_recv()
        emit(0, i)
    each_chunk(begin)

    def step(k, carry):
        p = lax.rem(k, 2)
        each_chunk(lambda i: total_norm(p, i))
        small(S_TO_SIB, p).start()
        small(S_TO_Y, p).start()
        each_chunk(lambda i: drive(p, i))
        mass[...] = jnp.zeros_like(mass)

        def arrive(i):
            copy(T_TO_Y, p, i).wait_recv()
            copy(FAR_TO_X, p, i).start()
            copy(FAR_TO_SIB, p, i).start()
            copy(T_TO_X, p, i).wait_recv()
            copy(OTHER_TO_SIB, p, i).start()
            row_norm(p, i)
        each_chunk(arrive)
        near_group(p, OWN)
        small(S_TO_Y, p).wait_recv()
        small(FAR_S_TO_SIB, p).start()
        far_arrive(p, 0)
        small(S_TO_SIB, p).wait_recv()

        def sib_ready(i):
            copy(T_TO_SIB, p, i).wait_recv()
            copy(OTHER_TO_SIB, p, i).wait_recv()
            copy(A_TO_SIB, p, i).wait_recv()
        each_chunk(sib_ready)
        near_group(p, SIB)
        far_arrive(p, 1)
        small(FAR_S_TO_SIB, p).wait_recv()

        def far_step(j, c):
            far_ready(p, j)
            each_chunk(lambda i: far_pair(p, i, j))

            @pl.when(j != 1)
            def _():
                far_arrive(p, 2 + j // 2)
            return c
        lax.fori_loop(0, chunks - 1, far_step, 0)
        far_ready(p, chunks - 1)

        def drain(i):
            for kind in range(11):
                copy(kind, p, i).wait_send()
        each_chunk(drain)
        for kind in range(3):
            small(kind, p).wait_send()

        def finish(i):
            far_pair(p, i, chunks - 1)
            total = jnp.sum(mass[span(i), :], axis=1, keepdims=True)
            theta[span(i), :] += pull_gain * total * tb[p, OWN, 0, span(i), :].astype(F32)

            @pl.when(k < NUM_STEPS - 1)
            def _():
                emit(1 - p, i)

            @pl.when(k == NUM_STEPS - 1)
            def _():
                store(i).start()
                give_back(i).start()
        each_chunk(finish)
        return carry
    lax.fori_loop(0, NUM_STEPS, step, 0)

    for kind in (FACTOR_TO_SIB, VECS_TO_SIB):
        table(kind).wait_send()

    def end(i):
        give(i).wait_send()
        store(i).wait()
        give_back(i).wait()
    each_chunk(end)


def solution(mesh):
    part_size = mesh.shape["part"]
    feat_size = mesh.shape["feat"]
    assert part_size == 2 and feat_size == 4

    def local_steps(local_theta, prec_loc, mean_loc, factor_loc):
        rows_loc, feat_loc = local_theta.shape
        n_total = rows_loc * part_size
        feat_total = feat_loc * feat_size
        kern_width = 2.0 * feat_total / math.log(n_total)
        step_size = 0.15 * n_total * feat_total / math.log(n_total)
        rows, feats = rows_loc // 2, feat_loc * 2
        chunks = rows // CHUNK
        assert chunks == 4
        rank = factor_loc.shape[1]
        vecs = jnp.concatenate([prec_loc[None], mean_loc[None], jnp.zeros((6, feat_loc), F32)], 0)

        vmem = pl.BlockSpec(memory_space=pltpu.VMEM)
        hbm = pl.BlockSpec(memory_space=pl.ANY)
        return pl.pallas_call(
            functools.partial(svgd_kernel, n_total, kern_width, step_size),
            out_shape=jax.ShapeDtypeStruct((rows_loc, feat_loc), F32),
            in_specs=[hbm, vmem, vmem],
            out_specs=hbm,
            scratch_shapes=[
                pltpu.VMEM((rows, feats), F32),
                pltpu.VMEM((8, feats), F32),
                pltpu.VMEM((rank, feats), BF16),
                pltpu.VMEM((2, 4, 2, rows, feats), BF16),
                pltpu.VMEM((2, 4, rows, feats), BF16),
                pltpu.VMEM((2, 2, rank + 8, rows), F32),
                pltpu.VMEM((2, 4, 8, rows), F32),
                pltpu.VMEM((rows, 128), F32),
                pltpu.VMEM((rows, 128), F32),
                pltpu.SemaphoreType.DMA((2, 11, chunks)),
                pltpu.SemaphoreType.DMA((2, 11, chunks)),
                pltpu.SemaphoreType.DMA((2, 3)),
                pltpu.SemaphoreType.DMA((2, 3)),
                pltpu.SemaphoreType.DMA((2, chunks)),
                pltpu.SemaphoreType.DMA((2, chunks)),
                pltpu.SemaphoreType.DMA((2, chunks)),
                pltpu.SemaphoreType.DMA((2,)),
                pltpu.SemaphoreType.DMA((2,)),
            ],
            compiler_params=pltpu.CompilerParams(
                collective_id=0, has_side_effects=True, vmem_limit_bytes=67043328),
            name="svgd_steps",
        )(local_theta, vecs, factor_loc.T)

    row_spec = P(("ens", "part"), "feat")
    vec_spec = P(("ens", "feat"))
    fac_spec = P(("ens", "feat"), None)
    return jax.shard_map(local_steps, mesh=mesh, in_specs=(row_spec, vec_spec, vec_spec, fac_spec), out_specs=row_spec, check_vma=False)
```

time: 2210 us -> 318 us (0.14)
  waiting for transfers between devices: 1820 us -> 0 us
  Pallas kernels: 0 us -> 312 us
  matrix products: 164 us -> 0 us
  blocking collectives: 126 us -> 0 us
  other arithmetic: 72.8 us -> 1.37 us
    psum x3 -> x0, waiting for transfers between devices: 1560 us -> none  [local_steps(): gram_rows, sq_norm = lax.psum((gram_part, sq_part), 'feat')]
    pallas_call x0 -> x1, Pallas kernels: none -> 312 us  [local_steps(): pl.pallas_call(functools.partial(svgd_kernel, n_total, kern_width, step_s...]
    all_gather x6 -> x0, waiting for transfers between devices: 266 us -> none  [the longest x3 165 us: local_steps(): theta_all = lax.all_gather(theta_b, 'part', axis=0, tiled=True)]
    dot_general x15 -> x0, matrix products: 164 us -> none  [the longest x3 53.7 us: local_steps(): jnp.einsum('nd,md->nm', theta_b, theta_all, preferred_element_type=jnp.fl...]
    psum x3 -> x0, blocking collectives: 126 us -> none  [local_steps(): gram_rows, sq_norm = lax.psum((gram_part, sq_part), 'feat')]
    reduce_sum x3 -> x0, other arithmetic: 66.4 us -> none  [local_steps(): row_mass = jnp.sum(kern_b, axis=1, dtype=jnp.float32)]
  transfers between devices with their start and end apart: 9 -> 0, of which waited for: 9 -> 0; matrix products, arithmetic and copies ran while one was open for 4% -> 0% of each run, Pallas kernels for 0% -> 0%
where the time goes in v1:
time: 318 us
  Pallas kernels  312 us (98%)
  local copies, waits for them, and re-layouts  4.72 us (1%)
    pallas_call x1, Pallas kernels, local_steps(): pl.pallas_call(functools.partial(svgd_kernel, n_total, kern_width, step_s...  312 us

profile of v1, /device:TPU:0, one launch (start us, length us, event | category | flops | bytes accessed | tf_op | source)
XLA Modules:
  0.0 318.0 jit_solution(8656368612360930758)
XLA Ops:
  0.0 0.1 pad.2.clone
  0.1 1.4 maximum_maximum_fusion.vecs_in
  1.5 311.9 %svgd_steps.1 = f32[2048,512]{1,0:T(8,128)} custom-call(f32[2048,512]{1,0:T(8,128)} %theta_in.1, f32[8,512]{1,0:T(8,128)} %maximum_maximum_fusion.vecs_in, bf16[16,512]{1,0:T(8,128)(2,1)} %bitcast.3), custom_call_target="tpu_custom_call" | custom-call | tf_op jit(solution)/shard_map/svgd_steps/pallas_call | solution.py:306
  313.3 4.6 %copy.6 = f32[2048,512]{1,0:T(8,128)} copy(f32[2048,512]{1,0:T(8,128)} %svgd_steps.1) | data formatting | bytes 8388608
  (1 shorter events, 0.0 us)

commit v2 on v1

--- a/solution.py
+++ b/solution.py
@@ -10,6 +10,7 @@
 NUM_STEPS = 3
 CHUNK = 256
 WIDE = 512
+TALL = 512
 F32 = jnp.float32
 BF16 = jnp.bfloat16
 MESH = pl.DeviceIdType.MESH
@@ -153,30 +154,31 @@
         total = jnp.sum(near * near + other * other, axis=1, keepdims=True)
         srow[span(i), :] = jnp.broadcast_to(total, (CHUNK, 128))
 
-    def tile(p, i, blocks, start, width):
+    def tile(p, i, blocks, start, width, height=TALL):
+        tall = pl.ds(pl.multiple_of(i * height, height), height)
         cols = pl.ds(pl.multiple_of(start, width), width)
         parts = []
         for block in blocks:
-            gram = dot_nt(tb[p, OWN, 0, span(i), :], tb[p, block, 0, cols, :])
-            gram = gram + dot_nt(tb[p, OWN, 1, span(i), :], tb[p, block, 1, cols, :])
-            sq_dist = jnp.maximum(srow[span(i), 0:1] + sb[p, block, 0:1, cols] - 2.0 * gram, 0.0)
+            gram = dot_nt(tb[p, OWN, 0, tall, :], tb[p, block, 0, cols, :])
+            gram = gram + dot_nt(tb[p, OWN, 1, tall, :], tb[p, block, 1, cols, :])
+            sq_dist = jnp.maximum(srow[tall, 0:1] + sb[p, block, 0:1, cols] - 2.0 * gram, 0.0)
             parts.append(jnp.exp(sq_dist * (-1.0 / kern_width)).astype(BF16))
         kern = jnp.concatenate(parts, axis=1)
         heavy = kern.astype(F32)
         lanes = heavy[:, 0:128]
         for q in range(1, kern.shape[1] // 128):
             lanes = lanes + heavy[:, q * 128:(q + 1) * 128]
-        mass[span(i), :] += lanes
+        mass[tall, :] += lanes
         push = dot_nn(kern, jnp.concatenate([ab[p, block, cols, :] for block in blocks], axis=0))
         pull = dot_nn(kern, jnp.concatenate([tb[p, block, 0, cols, :] for block in blocks], axis=0))
-        theta[span(i), :] += gain * push - pull_gain * pull
-
-    def near_group(p, block):
+        theta[tall, :] += gain * push - pull_gain * pull
+
+    def near_group(p, block, first, last):
         per_row = rows // WIDE
 
         def body(q):
             tile(p, q // per_row, (block,), lax.rem(q, per_row) * WIDE, WIDE)
-        lax.fori_loop(0, chunks * per_row, lambda q, c: (body(q), c)[1], 0)
+        lax.fori_loop(first, last, lambda q, c: (body(q), c)[1], 0)
 
     def far_pair(p, i, j):
         tile(p, i, (FAR, FAR_SIB), j * CHUNK, CHUNK)
@@ -210,6 +212,7 @@
 
     def step(k, carry):
         p = lax.rem(k, 2)
+        near_tiles = (rows // TALL) * (rows // WIDE)
         each_chunk(lambda i: total_norm(p, i))
         small(S_TO_SIB, p).start()
         small(S_TO_Y, p).start()
@@ -223,8 +226,12 @@
             copy(T_TO_X, p, i).wait_recv()
             copy(OTHER_TO_SIB, p, i).start()
             row_norm(p, i)
+
+            @pl.when(i == 1)
+            def _():
+                near_group(p, OWN, 0, 1)
         each_chunk(arrive)
-        near_group(p, OWN)
+        near_group(p, OWN, 1, near_tiles)
         small(S_TO_Y, p).wait_recv()
         small(FAR_S_TO_SIB, p).start()
         far_arrive(p, 0)
@@ -235,13 +242,13 @@
             copy(OTHER_TO_SIB, p, i).wait_recv()
             copy(A_TO_SIB, p, i).wait_recv()
         each_chunk(sib_ready)
-        near_group(p, SIB)
+        near_group(p, SIB, 0, near_tiles)
         far_arrive(p, 1)
         small(FAR_S_TO_SIB, p).wait_recv()
 
         def far_step(j, c):
             far_ready(p, j)
-            each_chunk(lambda i: far_pair(p, i, j))
+            lax.fori_loop(0, rows // TALL, lambda i, d: (far_pair(p, i, j), d)[1], 0)
 
             @pl.when(j != 1)
             def _():
@@ -258,7 +265,7 @@
             small(kind, p).wait_send()
 
         def finish(i):
-            far_pair(p, i, chunks - 1)
+            tile(p, i, (FAR, FAR_SIB), (chunks - 1) * CHUNK, CHUNK, CHUNK)
             total = jnp.sum(mass[span(i), :], axis=1, keepdims=True)
             theta[span(i), :] += pull_gain * total * tb[p, OWN, 0, span(i), :].astype(F32)
 

time: 318 us -> 315 us (level)
  no operation moved by 1% of the time
where the time goes in v2:
time: 315 us
  Pallas kernels  309 us (98%)
  local copies, waits for them, and re-layouts  4.72 us (1%)
    pallas_call x1, Pallas kernels, local_steps(): pl.pallas_call(functools.partial(svgd_kernel, n_total, kern_width, step_s...  309 us

profile of v2, /device:TPU:0, one launch (start us, length us, event | category | flops | bytes accessed | tf_op | source)
XLA Modules:
  0.0 315.1 jit_solution(2673678014188385928)
XLA Ops:
  0.0 0.1 pad.2.clone
  0.1 1.4 maximum_maximum_fusion.vecs_in
  1.5 309.0 %svgd_steps.1 = f32[2048,512]{1,0:T(8,128)} custom-call(f32[2048,512]{1,0:T(8,128)} %theta_in.1, f32[8,512]{1,0:T(8,128)} %maximum_maximum_fusion.vecs_in, bf16[16,512]{1,0:T(8,128)(2,1)} %bitcast.3), custom_call_target="tpu_custom_call" | custom-call | tf_op jit(solution)/shard_map/svgd_steps/pallas_call | solution.py:313
  310.5 4.6 %copy.6 = f32[2048,512]{1,0:T(8,128)} copy(f32[2048,512]{1,0:T(8,128)} %svgd_steps.1) | data formatting | bytes 8388608
  (1 shorter events, 0.0 us)
